TPU v7x, 512 devices: a whole 4x8x8 slice. The times are simulated.
512 devices in a mesh: tile: 64 (over z, x, core), mem: 8 (over y).
Axes of the slice: x: 4, y: 8, z: 8, core: 2. Of those that a mesh axis runs over, the one named last changes fastest.
Arguments:
- anomalies: bfloat16 [80, 137, 8192], P('mem', None, 'tile'), may hold values from -6 to 6
- analysis_weights: bfloat16 [64, 80, 80], P('tile'), may hold values from -0.6 to 1.7
- background_mean: bfloat16 [137, 8192], P(None, 'tile'), may hold values from -6 to 6
- background: bfloat16 [80, 137, 8192], P('mem', None, 'tile'), may hold values from -6 to 6
- jacobian_table: bfloat16 [8461, 137], replicated, may hold values from -0.5 to 0.5
- channel_list: int32 [96], replicated, may hold values from 0 to 8460
- send_slots: int32 [64, 64, 32], P('tile'), may hold values from -1 to 127, as said below
- footprint: int32 [32768, 4], P('tile'), may hold values from 0 to 2047, as said below
- footprint_weight: bfloat16 [32768, 4], P('tile'), may hold values from 0.25 to 1
- channel_bias: float32 [96], replicated, may hold values from -4 to 4
Outputs:
- analysis_members: bfloat16 [80, 137, 8192], P('mem', None, 'tile')
- radiance_prior: float32 [96, 80, 32768], P(None, 'mem', 'tile')
Inputs may be any that keep to these rules, and one draw needn't show every extreme that they name: `send_slots`: entry [s, d, i] is a column within owner s's block of 128 columns that owner s sends to tile d in slot i, or -1 for an empty slot; the filled slots of a pair come first, each pair fills 1 to 32 slots, and in every draw one tile receives 32 filled slots from every owner. `footprint`: entry [o, j] is a slot of the buffer of observation o's tile, which holds 32 slots from each owner in owner order; every entry names a filled slot, the 4 entries of a row differ, and every filled slot is named by some row of that tile.
All inputs are finite; a program needn't handle non-finite values.
Results may differ from a plain program's by a relative error of at most 0.0021.
Values may be sent and summed in bfloat16 or wider, within the bound.
No kernel may reach another device: no remote copies, remote signals or barrier semaphores. Data moves between devices by JAX's collectives and lax.ppermute only.
A program may use at most 128 MiB of HBM per device.

v0:
```python
import jax
import jax.numpy as jnp
from jax import lax
from jax.sharding import PartitionSpec as P

GROUP = 128
FOOT = 4


def shards(
    anomalies,
    analysis_weights,
    background_mean,
    background,
    jacobian_table,
    channel_list,
    send_slots,
    footprint,
    footprint_weight,
    channel_bias,
):
    mem_dev = anomalies.shape[0]
    levels = anomalies.shape[1]
    columns_dev = anomalies.shape[2]
    groups = columns_dev // GROUP
    mean_float = background_mean.astype(jnp.float32)
    member_start = lax.axis_index("mem") * mem_dev
    member_piece = lax.all_gather(anomalies, "mem", axis=0, tiled=True)
    piece_rows = member_piece.shape[0]
    weight_rows = analysis_weights
    weight_rows = lax.dynamic_slice_in_dim(weight_rows, member_start, mem_dev, 2)
    reshaped = member_piece.reshape(piece_rows, levels, groups, GROUP)
    mixture = jnp.einsum(
        "klgc,gkm->mlgc", reshaped, weight_rows, preferred_element_type=jnp.float32
    )
    analysis_members = (mixture.reshape(mem_dev, levels, columns_dev) + mean_float[None]).astype(
        jnp.bfloat16
    )
    selected = jnp.take(jacobian_table, channel_list, axis=0)
    slot_cols = jnp.maximum(send_slots[0], 0).reshape(-1)
    owned = jnp.einsum(
        "cl,klx->ckx", selected, background, preferred_element_type=jnp.float32
    ).astype(jnp.bfloat16)
    packed = jnp.take(owned, slot_cols, axis=2)
    received = lax.all_to_all(packed, "tile", split_axis=2, concat_axis=2, tiled=True)
    channels = received.shape[0]
    obs_count = footprint.shape[0]
    picked = jnp.take(received, footprint.reshape(-1), axis=2).reshape(
        channels, mem_dev, obs_count, FOOT
    )
    weighted = picked.astype(jnp.float32) * footprint_weight.astype(jnp.float32)[None, None]
    prior_out = jnp.sum(weighted, axis=3) + channel_bias[:, None, None]
    return (analysis_members, prior_out)


def solution(mesh):
    placed = (
        P("mem", None, "tile"),
        P("tile", None, None),
        P(None, "tile"),
        P("mem", None, "tile"),
        P(),
        P(),
        P("tile", None, None),
        P("tile", None),
        P("tile", None),
        P(),
    )
    return jax.shard_map(
        shards,
        mesh=mesh,
        in_specs=placed,
        out_specs=(P("mem", None, "tile"), P(None, "mem", "tile")),
        check_vma=False,
    )
```

profile of v0, /device:TPU:40, one launch (start us, length us, event | category | flops | bytes accessed | tf_op | source)
XLA Modules:
  0.0 244.1 jit_solution(10561270213525522859)
XLA Ops:
  7.2 0.7 compare_select_fusion.2
  7.9 0.7 compare_and_fusion.1
  8.5 0.7 broadcast_maximum_fusion
  9.3 0.7 broadcast_compare_fusion
  10.0 5.6 %copy.35 = bf16[8461,137]{1,0:T(8,128)(2,1)} copy(bf16[8461,137]{0,1:T(8,128)(2,1)} %param.14) | data formatting | bytes 4636628 | tf_op args[4]
  15.6 3.5 %gather_fusion = bf16[96,137]{1,0:T(8,128)(2,1)S(1)} fusion(bf16[8461,137]{1,0:T(8,128)(2,1)} %copy.35, s32[1024]{0:T(1024)S(1)} %pad_clamp_fusion), kind=kCustom, calls=%fused_computation | custom fusion | bytes 52992 | tf_op jit(solution)/shard_map/jit(_take)/gather | solution.py:39
  19.1 0.3 convolution_convert_fusion
  19.3 0.4 copy.38
  19.8 0.1 copy.37
  19.9 0.1 reshape.96
  19.9 0.1 copy.34
  20.0 0.1 le.39
  20.1 16.2 %gather_fusion.1 = bf16[2048,96,10]{1,2,0:T(8,128)(2,1)} fusion(bf16[96,10,128]{0,1,2:T(8,128)(2,1)S(1)} %copy.38, s32[2048]{0:T(1024)S(1)} %broadcast_clamp_fusion.1), kind=kCustom, calls=%fused_computation.1 | custom fusion | bytes 7872512 | tf_op jit(solution)/shard_map/jit(_take)/gather | solution.py:44
  36.4 9.4 %fusion.16 = bf16[2048,10,96]{2,1,0:T(8,128)(2,1)} fusion(bf16[2048,96,10]{1,2,0:T(8,128)(2,1)} %gather_fusion.1, pred[2048]{0:T(1024)(128)(4,1)S(1)} %le.39), kind=kLoop, calls=%fused_computation.29 | loop fusion | flops 1966080 | bytes 7866368
  45.8 15.3 %reshape.114 = bf16[64,2,15360]{2,1,0:T(2,128)(2,1)} reshape(bf16[2048,10,96]{2,1,0:T(8,128)(2,1)} %fusion.16) | data formatting | bytes 7864320
  61.1 14.2 %all-to-all-start = ((bf16[64,2,15360]{2,1,0:T(2,128)(2,1)}), bf16[64,2,15360]{2,1,0:T(2,128)(2,1)}, u32[]{:S(2)}, u32[]{:S(2)}) async-start(bf16[64,2,15360]{2,1,0:T(2,128)(2,1)} %reshape.114), calls=%async_computation | async-start | bytes 7864320 | tf_op jit(solution)/shard_map/all_to_all | solution.py:45
  75.3 0.2 all-gather.2.cloned.1.call-start
  75.5 0.5 all-gather.2.cloned.1.call-update
  76.1 0.1 copy.39
  76.2 0.2 reshape.85
  76.4 0.1 copy.41
  76.6 0.2 copy.33
  76.8 46.1 %all-gather.2.cloned.1.call-done = bf16[80,137,128]{2,1,0:T(8,128)(2,1)} async-done(((bf16[10,137,128]{2,1,0:T(8,128)(2,1)}), bf16[80,137,128]{2,1,0:T(8,128)(2,1)}) %all-gather.2.cloned.1.call-update) | async-done | bytes 2805776 | tf_op jit(solution)/shard_map/all_gather | solution.py:28
  122.9 2.5 %fusion.5 = bf16[10,137,128]{2,0,1:T(8,128)(2,1)S(1)} fusion(bf16[80,137,128]{2,1,0:T(8,128)(2,1)} %all-gather.2.cloned.1.call-done, f32[137,128]{1,0:T(8,128)S(1)} %convert_element_type.15, bf16[1,80,80]{2,1,0:T(8,128)(2,1)S(1)} %copy-done.3, s32[]{:T(128)S(6)} %select_n.43), kind=kOutput, calls=%fused_computation.8 | convolution fusion | flops 28408320 | bytes 3239428 | tf_op jit(solution)/shard_map/klgc,gkm->mlgc/dot_general | solution.py:33
  125.4 0.8 copy.42
  126.3 39.7 %all-to-all-done = bf16[64,2,15360]{2,1,0:T(2,128)(2,1)} async-done(((bf16[64,2,15360]{2,1,0:T(2,128)(2,1)}), bf16[64,2,15360]{2,1,0:T(2,128)(2,1)}, u32[]{:S(2)}, u32[]{:S(2)}) %all-to-all-start) | async-done | bytes 3932192 | tf_op jit(solution)/shard_map/all_to_all | solution.py:45
  165.9 15.2 %reshape.115 = bf16[2048,10,96]{2,1,0:T(8,128)(2,1)} reshape(bf16[64,2,15360]{2,1,0:T(2,128)(2,1)} %all-to-all-done) | data formatting | bytes 7864320
  181.1 19.6 %gather_fusion.2 = bf16[2048,96,10]{1,2,0:T(8,128)(2,1)} fusion(bf16[96,10,2048]{0,1,2:T(8,128)(2,1)} %bitcast.19, s32[2048]{0:T(1024)S(1)} %broadcast_clamp_fusion), kind=kCustom, calls=%fused_computation.2 | custom fusion | bytes 7872512 | tf_op jit(solution)/shard_map/jit(_take)/gather | solution.py:48
  200.7 4.7 %copy.40 = bf16[96,10,2048]{0,2,1:T(8,128)(2,1)S(1)} copy(bf16[96,10,2048]{0,1,2:T(8,128)(2,1)} %bitcast.20) | data formatting | bytes 7864320 | tf_op jit(solution)/shard_map/jit(_take)/gather | solution.py:48
  205.5 29.6 %multiply_reduce_fusion = f32[96,10,512]{0,2,1:T(8,128)S(1)} fusion(f32[512,4]{1,0:T(8,128)S(1)} %copy.41, bf16[96,10,512,4]{0,3,2,1:T(4,128)(2,1)S(1)} %bitcast.21, pred[512,4]{1,0:T(8,128)(4,1)S(1)} %copy.33), kind=kLoop, calls=%fused_computation.3 | loop fusion | flops 7372800 | bytes 5908480 | tf_op jit(solution)/shard_map/reduce_sum | solution.py:52
  235.1 0.2 broadcast_add_fusion
  235.3 1.9 copy.43
  (18 shorter events, 0.1 us)
Async XLA Ops:
  7.2 11.9 %copy-start = (bf16[10,137,128]{2,1,0:T(8,128)(2,1)S(1)}, bf16[10,137,128]{2,1,0:T(8,128)(2,1)}, u32[]{:S(2)}) copy-start(bf16[10,137,128]{2,1,0:T(8,128)(2,1)} %param.13) | copy-start | bytes 1052164
  61.1 14.9 %copy-start.1 = (bf16[137,128]{1,0:T(8,128)(2,1)S(1)}, bf16[137,128]{1,0:T(8,128)(2,1)}, u32[]{:S(2)}) copy-start(bf16[137,128]{1,0:T(8,128)(2,1)} %param.12) | copy-start | bytes 105220
  61.1 14.9 %copy-start.2 = (s32[512,4]{0,1:T(4,128)S(1)}, s32[512,4]{0,1:T(4,128)}, u32[]{:S(2)}) copy-start(s32[512,4]{0,1:T(4,128)} %param.17) | copy-start | bytes 24580
  61.1 15.3 %copy-start.4 = (bf16[512,4]{0,1:T(4,128)(2,1)S(1)}, bf16[512,4]{0,1:T(4,128)(2,1)}, u32[]{:S(2)}) copy-start(bf16[512,4]{0,1:T(4,128)(2,1)} %param.18) | copy-start | bytes 12292
  61.1 61.8 %copy-start.3 = (bf16[1,80,80]{2,1,0:T(8,128)(2,1)S(1)}, bf16[1,80,80]{2,1,0:T(8,128)(2,1)}, u32[]{:S(2)}) copy-start(bf16[1,80,80]{2,1,0:T(8,128)(2,1)} %param.11) | copy-start | bytes 38404
  61.1 104.8 %all-to-all-start = ((bf16[64,2,15360]{2,1,0:T(2,128)(2,1)}), bf16[64,2,15360]{2,1,0:T(2,128)(2,1)}, u32[]{:S(2)}, u32[]{:S(2)}) async-start(bf16[64,2,15360]{2,1,0:T(2,128)(2,1)} %reshape.114), calls=%async_computation | async-start | bytes 7864320 | tf_op jit(solution)/shard_map/all_to_all | solution.py:45
  75.3 47.6 %all-gather.2.cloned.1.call-start = ((), (), s32[]{:S(2)}) async-start(), calls=%async_computation.1 | async-start | bytes 3317760 | tf_op jit(solution)/shard_map/all_gather | solution.py:28
  205.4 29.6 %copy-start.5 = (f32[96]{0:T(128)S(1)}, f32[96]{0:T(128)}, u32[]{:S(2)}) copy-start(f32[96]{0:T(128)} %param.19) | copy-start | bytes 1156
Sparse Core Ops, SparseCore 0:
  78.2 44.6 all-gather.1
where the time goes:
time: 245 us; the launch traced here: 244 us
  waiting for transfers between devices  86.2 us (35%)
  local copies, waits for them, and re-layouts  84.4 us (34%)
  other arithmetic  42.1 us (17%)
  starting transfers between devices  14.4 us (6%)
  between operations  14.2 us (6%)
  matrix products  2.81 us (1%)
    all_gather x1, waiting for transfers between devices, shards(): member_piece = lax.all_gather(anomalies, 'mem', axis=0, tiled=True)  46.1 us
    all_to_all x1, waiting for transfers between devices, shards(): lax.all_to_all(packed, 'tile', split_axis=2, concat_axis=2, tiled=True)  39.7 us
    unnamed x18, local copies, waits for them, and re-layouts  39 us
    reduce_sum x1, other arithmetic, shards(): prior_out = jnp.sum(weighted, axis=3) + channel_bias[:, None, None]  29.6 us
    gather x2, local copies, waits for them, and re-layouts, shards(): jnp.take(received, footprint.reshape(-1), axis=2)  24.3 us
    gather x1, local copies, waits for them, and re-layouts, shards(): packed = jnp.take(owned, slot_cols, axis=2)  16.2 us
    all_to_all x1, starting transfers between devices, shards(): lax.all_to_all(packed, 'tile', split_axis=2, concat_axis=2, tiled=True)  14.2 us
    unnamed x1, other arithmetic  9.41 us
  transfers between devices with their start and end apart: 2, of which 2 were waited for; matrix products, arithmetic and copies ran while one was open for 2% of the time, Pallas kernels for 0%

commit v1 on v0

v1 whole, which is shorter than its diff:
```python
import jax
import jax.numpy as jnp
from jax import lax
from jax.sharding import PartitionSpec as P

SLOTS = 32
FOOT = 4
f32 = jnp.float32
bf16 = jnp.bfloat16


def shards(
    anomalies,
    analysis_weights,
    background_mean,
    background,
    jacobian_table,
    channel_list,
    send_slots,
    footprint,
    footprint_weight,
    channel_bias,
):
    mem_dev, levels, cols = anomalies.shape
    spectrum = jacobian_table.shape[0]
    channels = channel_list.shape[0]
    tiles = send_slots.shape[1]
    obs = footprint.shape[0]
    n_mem = lax.axis_size("mem")
    members = n_mem * mem_dev
    feats = mem_dev * channels

    pick = (channel_list[:, None] == lax.broadcasted_iota(jnp.int32, (channels, spectrum), 1)).astype(bf16)
    selected = jnp.einsum("cv,vl->cl", pick, jacobian_table, preferred_element_type=f32).astype(bf16)
    owned = jnp.einsum("klx,cl->xkc", background, selected, preferred_element_type=f32).astype(bf16)
    owned = owned.reshape(cols, feats)
    slots = jnp.maximum(send_slots[0], 0)
    slot_pick = (slots[:, :, None] == lax.broadcasted_iota(jnp.int32, (tiles, SLOTS, cols), 2)).astype(bf16)
    packed = jnp.einsum("dsx,xf->dsf", slot_pick, owned, preferred_element_type=f32).astype(bf16)
    received = lax.all_to_all(packed, "tile", 0, 0)

    block = -(-levels // n_mem)
    padded = jnp.pad(anomalies, ((0, 0), (0, block * n_mem - levels), (0, 0)))
    pieces = padded.reshape(mem_dev, n_mem, block, cols).transpose(1, 0, 2, 3).reshape(n_mem, mem_dev * block, cols)
    pieces = lax.all_to_all(pieces, "mem", 0, 0).reshape(members, block, cols)
    mixed = jnp.einsum("klc,km->mlc", pieces, analysis_weights[0], preferred_element_type=f32)
    mean = jnp.pad(background_mean, ((0, block * n_mem - levels), (0, 0)))
    mean = lax.dynamic_slice_in_dim(mean, lax.axis_index("mem") * block, block, 0)
    done = (mixed + mean.astype(f32)[None]).astype(bf16).reshape(n_mem, mem_dev * block, cols)
    done = lax.all_to_all(done, "mem", 0, 0).reshape(n_mem, mem_dev, block, cols)
    analysis_members = done.transpose(1, 0, 2, 3).reshape(mem_dev, n_mem * block, cols)[:, :levels]

    rows = lax.broadcasted_iota(jnp.int32, (tiles * SLOTS, obs), 0)
    weight = jnp.zeros((tiles * SLOTS, obs), f32)
    for j in range(FOOT):
        weight = jnp.where(rows == footprint[:, j][None], footprint_weight[:, j].astype(f32)[None], weight)
    prior = jnp.einsum(
        "sf,so->fo", received.reshape(tiles * SLOTS, feats), weight.astype(bf16), preferred_element_type=f32
    )
    prior = prior.reshape(mem_dev, channels, obs) + channel_bias[None, :, None]
    return (analysis_members, prior.transpose(1, 0, 2))


def solution(mesh):
    placed = (
        P("mem", None, "tile"),
        P("tile", None, None),
        P(None, "tile"),
        P("mem", None, "tile"),
        P(),
        P(),
        P("tile", None, None),
        P("tile", None),
        P("tile", None),
        P(),
    )
    return jax.shard_map(
        shards,
        mesh=mesh,
        in_specs=placed,
        out_specs=(P("mem", None, "tile"), P(None, "mem", "tile")),
        check_vma=False,
    )
```

time: 245 us -> 166 us (0.68)
  the two profiles are of different devices: /device:TPU:40 before, /device:TPU:2 now
where the time goes in v1:
time: 166 us; the launch traced here: 165 us
  waiting for transfers between devices  118 us (71%)
  starting transfers between devices  24.6 us (15%)
  matrix products  11.2 us (7%)
  local copies, waits for them, and re-layouts  10.7 us (6%)
    all_to_all x1, waiting for transfers between devices, shards(): received = lax.all_to_all(packed, 'tile', 0, 0)  95 us
    all_to_all x1, waiting for transfers between devices, shards(): pieces = lax.all_to_all(pieces, 'mem', 0, 0).reshape(members, block, cols)  14.3 us
    all_to_all x1, starting transfers between devices, shards(): received = lax.all_to_all(packed, 'tile', 0, 0)  14.1 us
    all_to_all x1, waiting for transfers between devices, shards(): lax.all_to_all(done, 'mem', 0, 0).reshape(n_mem, mem_dev, block, cols)  8.49 us
    all_to_all x1, starting transfers between devices, shards(): pieces = lax.all_to_all(pieces, 'mem', 0, 0).reshape(members, block, cols)  7.1 us
    dot_general x1, local copies, waits for them, and re-layouts, shards(): jnp.einsum('sf,so->fo', received.reshape(tiles * SLOTS, feats), weight.as...  6.35 us
    dot_general x1, matrix products, shards(): jnp.einsum('sf,so->fo', received.reshape(tiles * SLOTS, feats), weight.as...  5.75 us
    all_to_all x1, starting transfers between devices, shards(): lax.all_to_all(done, 'mem', 0, 0).reshape(n_mem, mem_dev, block, cols)  3.45 us
  transfers between devices with their start and end apart: 3, of which 3 were waited for; matrix products, arithmetic and copies ran while one was open for 4% of the time, Pallas kernels for 0%

profile of v1, /device:TPU:2, one launch (start us, length us, event | category | flops | bytes accessed | tf_op | source)
XLA Modules:
  0.0 165.2 jit_solution(10701485742385134220)
XLA Ops:
  0.6 0.0 copy-start
  0.6 0.0 copy-start.1
  0.7 0.0 copy-start.2
  0.7 1.2 pad.8
  1.8 0.1 reshape.72
  2.0 0.0 copy-start.3
  2.0 0.0 copy-start.6
  2.0 0.1 copy.24
  2.0 0.8 copy.25
  2.8 7.1 %all-to-all-start = ((bf16[8,180,128]{2,1,0:T(8,128)(2,1)}), bf16[8,180,128]{2,1,0:T(8,128)(2,1)S(1)}, u32[]{:S(2)}, u32[]{:S(2)}) async-start(bf16[8,180,128]{2,1,0:T(8,128)(2,1)} %copy.25), calls=%async_computation | async-start | bytes 753664 | tf_op jit(solution)/shard_map/all_to_all | solution.py:45
  9.9 0.0 copy-done.1
  10.0 14.3 %all-to-all-done = bf16[8,180,128]{2,1,0:T(8,128)(2,1)S(1)} async-done(((bf16[8,180,128]{2,1,0:T(8,128)(2,1)}), bf16[8,180,128]{2,1,0:T(8,128)(2,1)S(1)}, u32[]{:S(2)}, u32[]{:S(2)}) %all-to-all-start) | async-done | bytes 368672 | tf_op jit(solution)/shard_map/all_to_all | solution.py:45
  24.3 0.1 reshape.74
  24.4 0.0 copy-done.2
  24.4 0.3 fusion.17
  24.7 0.1 copy.28
  24.8 0.9 reshape.75
  25.7 3.4 %all-to-all-start.1 = ((bf16[8,180,128]{2,1,0:T(8,128)(2,1)}), bf16[8,180,128]{2,1,0:T(8,128)(2,1)S(1)}, u32[]{:S(2)}, u32[]{:S(2)}) async-start(bf16[8,180,128]{2,1,0:T(8,128)(2,1)} %reshape.75), calls=%async_computation.1 | async-start | bytes 753664 | tf_op jit(solution)/shard_map/all_to_all | solution.py:50
  29.1 0.0 copy-done.3
  29.2 0.1 copy.31
  29.2 0.0 copy-done
  29.3 2.2 %convolution_convert_fusion.1 = bf16[96,10,128]{2,0,1:T(8,128)(2,1)S(1)} fusion(bf16[10,137,128]{2,1,0:T(8,128)(2,1)} %param.13, bf16[8461,137]{0,1:T(8,128)(2,1)S(1)} %copy-done, s32[96]{0:T(128)S(1)} %copy-done.6), kind=kOutput, calls=%fused_computation.23 | convolution fusion | flops 257175552 | bytes 2915178 | tf_op jit(solution)/shard_map/klx,cl->xkc/dot_general | solution.py:35
  31.5 2.9 %convolution_convert_fusion = bf16[64,32,960]{2,1,0:T(8,128)(2,1)} fusion(bf16[128,960,1]{0,1,2:T(8,128)(2,1)S(1)} %bitcast.52, s32[64,32]{1,0:T(8,128)S(1)} %copy.31), kind=kOutput, calls=%fused_computation.7 | convolution fusion | flops 505544704 | bytes 4186112 | tf_op jit(solution)/shard_map/dsx,xf->dsf/dot_general | solution.py:39
  34.4 8.5 %all-to-all-done.1 = bf16[8,180,128]{2,1,0:T(8,128)(2,1)S(1)} async-done(((bf16[8,180,128]{2,1,0:T(8,128)(2,1)}), bf16[8,180,128]{2,1,0:T(8,128)(2,1)S(1)}, u32[]{:S(2)}, u32[]{:S(2)}) %all-to-all-start.1) | async-done | bytes 368672 | tf_op jit(solution)/shard_map/all_to_all | solution.py:50
  42.9 14.1 %all-to-all-start.2 = ((bf16[64,32,960]{2,1,0:T(8,128)(2,1)}), bf16[64,32,960]{2,1,0:T(8,128)(2,1)}, u32[]{:S(2)}, u32[]{:S(2)}) async-start(bf16[64,32,960]{2,1,0:T(8,128)(2,1)} %convolution_convert_fusion), calls=%async_computation.2 | async-start | bytes 8388608 | tf_op jit(solution)/shard_map/all_to_all | solution.py:40
  57.0 0.0 copy-done.4
  57.0 0.1 copy.29
  57.1 0.1 copy.30
  57.2 0.9 reshape.77
  58.0 95.0 %all-to-all-done.2 = bf16[64,32,960]{2,1,0:T(8,128)(2,1)} async-done(((bf16[64,32,960]{2,1,0:T(8,128)(2,1)}), bf16[64,32,960]{2,1,0:T(8,128)(2,1)}, u32[]{:S(2)}, u32[]{:S(2)}) %all-to-all-start.2) | async-done | bytes 3932192 | tf_op jit(solution)/shard_map/all_to_all | solution.py:40
  153.1 6.3 %copy.32 = bf16[960,2048]{1,0:T(8,128)(2,1)} copy(bf16[960,2048]{0,1:T(8,128)(2,1)} %bitcast.13) | data formatting | bytes 7864320 | tf_op jit(solution)/shard_map/sf,so->fo/dot_general | solution.py:57
  159.4 5.7 %add_bitcast_fusion = f32[96,10,512]{2,0,1:T(8,128)} fusion(bf16[10,96,2048]{2,1,0:T(8,128)(2,1)} %bitcast.47, f32[512]{0:T(512)S(1)} %bitcast.55, s32[512]{0:T(512)S(1)} %bitcast.59, f32[512]{0:T(512)S(1)} %bitcast.56, s32[512]{0:T(512)S(1)} %bitcast.60, f32[512]{0:T(512)S(1)} %bitcast.54, s32[512]{0:T(512)S(1)} %bitcast.58, f32[512]{0:T(512)S(1)} %bitcast.53, ...), kind=kOutput, calls=%fused_computation.19 | convolution fusion | flops 2022146048 | bytes 5915008 | tf_op jit(solution)/shard_map/sf,so->fo/dot_general | solution.py:57
  (10 shorter events, 0.1 us)
Async XLA Ops:
  0.6 28.6 %copy-start = (bf16[8461,137]{0,1:T(8,128)(2,1)S(1)}, bf16[8461,137]{0,1:T(8,128)(2,1)}, u32[]{:S(2)}) copy-start(bf16[8461,137]{0,1:T(8,128)(2,1)} %param.14) | copy-start | bytes 6954946
  0.6 9.3 %copy-start.1 = (bf16[137,128]{1,0:T(8,128)(2,1)S(1)}, bf16[137,128]{1,0:T(8,128)(2,1)}, u32[]{:S(2)}) copy-start(bf16[137,128]{1,0:T(8,128)(2,1)} %param.12) | copy-start | bytes 105220
  0.7 23.7 %copy-start.2 = (bf16[1,80,80]{2,1,0:T(8,128)(2,1)S(1)}, bf16[1,80,80]{2,1,0:T(8,128)(2,1)}, u32[]{:S(2)}) copy-start(bf16[1,80,80]{2,1,0:T(8,128)(2,1)} %param.11) | copy-start | bytes 38404
  2.0 27.2 %copy-start.3 = (s32[1,64,32]{1,2,0:T(8,128)S(1)}, s32[1,64,32]{1,2,0:T(8,128)}, u32[]{:S(2)}) copy-start(s32[1,64,32]{1,2,0:T(8,128)} %param.16) | copy-start | bytes 24580
  2.0 27.3 %copy-start.6 = (s32[96]{0:T(128)S(1)}, s32[96]{0:T(128)}, u32[]{:S(2)}) copy-start(s32[96]{0:T(128)} %param.15) | copy-start | bytes 1156
  2.8 21.4 %all-to-all-start = ((bf16[8,180,128]{2,1,0:T(8,128)(2,1)}), bf16[8,180,128]{2,1,0:T(8,128)(2,1)S(1)}, u32[]{:S(2)}, u32[]{:S(2)}) async-start(bf16[8,180,128]{2,1,0:T(8,128)(2,1)} %copy.25), calls=%async_computation | async-start | bytes 753664 | tf_op jit(solution)/shard_map/all_to_all | solution.py:45
  25.7 17.2 %all-to-all-start.1 = ((bf16[8,180,128]{2,1,0:T(8,128)(2,1)}), bf16[8,180,128]{2,1,0:T(8,128)(2,1)S(1)}, u32[]{:S(2)}, u32[]{:S(2)}) async-start(bf16[8,180,128]{2,1,0:T(8,128)(2,1)} %reshape.75), calls=%async_computation.1 | async-start | bytes 753664 | tf_op jit(solution)/shard_map/all_to_all | solution.py:50
  34.4 22.6 %copy-start.4 = (bf16[512,4]{0,1:T(4,128)(2,1)S(1)}, bf16[512,4]{0,1:T(4,128)(2,1)}, u32[]{:S(2)}) copy-start(bf16[512,4]{0,1:T(4,128)(2,1)} %param.18) | copy-start | bytes 12292
  34.4 22.6 %copy-start.5 = (s32[512,4]{0,1:T(4,128)S(1)}, s32[512,4]{0,1:T(4,128)}, u32[]{:S(2)}) copy-start(s32[512,4]{0,1:T(4,128)} %param.17) | copy-start | bytes 24580
  42.9 110.2 %all-to-all-start.2 = ((bf16[64,32,960]{2,1,0:T(8,128)(2,1)}), bf16[64,32,960]{2,1,0:T(8,128)(2,1)}, u32[]{:S(2)}, u32[]{:S(2)}) async-start(bf16[64,32,960]{2,1,0:T(8,128)(2,1)} %convolution_convert_fusion), calls=%async_computation.2 | async-start | bytes 8388608 | tf_op jit(solution)/shard_map/all_to_all | solution.py:40
  153.1 6.4 %copy-start.7 = (f32[96]{0:T(128)S(1)}, f32[96]{0:T(128)}, u32[]{:S(2)}) copy-start(f32[96]{0:T(128)} %param.19) | copy-start | bytes 1156
